TPU v7x, 128 devices: a whole 4x4x4 slice. The times are simulated.
128 devices in a mesh: dp: 1, cp: 128 (over z, y, x, core).
Axes of the slice: x: 4, y: 4, z: 4, core: 2. Of those that a mesh axis runs over, the one named last changes fastest.
Arguments:
- hidden: bfloat16 [16384, 4096], P(('dp', 'cp'))
- grad_out: bfloat16 [16384, 4096], P(('dp', 'cp'))
- w_query: bfloat16 [4096, 8, 128], replicated
- w_key: bfloat16 [4096, 2, 128], replicated
- w_value: bfloat16 [4096, 2, 128], replicated
- w_out: bfloat16 [8, 128, 4096], replicated
Outputs:
- output 1: bfloat16 [16384, 4096], P(('dp', 'cp'))
- output 2: bfloat16 [16384, 4096], P(('dp', 'cp'))
- output 3: float32 [4096, 8, 128], P('dp')
- output 4: float32 [4096, 2, 128], P('dp')
- output 5: float32 [4096, 2, 128], P('dp')
- output 6: float32 [8, 128, 4096], P('dp')
All inputs are finite; a program needn't handle non-finite values.
Results may differ from a plain program's by a relative error of at most 0.010151.
Values are sent between devices in bfloat16 or wider.
A program may use at most 1 GiB of HBM per device.

v0:
```python
import jax
import jax.numpy as jnp
from jax import lax
from jax.sharding import PartitionSpec as P


def token_positions(groups, tok_local):
    half_len = tok_local // 2
    row_ids = jnp.arange(groups * tok_local)
    owner_dev = row_ids // tok_local
    within = row_ids % tok_local
    block_idx = jnp.where(within < half_len, owner_dev, 2 * groups - 1 - owner_dev)
    return block_idx * half_len + within % half_len


def solution(mesh):
    groups = mesh.shape["cp"]
    row_spec = P(("dp", "cp"), None)
    rep_spec = P(None, None, None)
    part_spec = P("dp", None, None)

    def device_layer(hidden, grad_out, w_query, w_key, w_value, w_out):
        tok_local, model_width = hidden.shape
        num_heads, head_dim = w_query.shape[1], w_query.shape[2]
        kv_heads = w_key.shape[1]
        group_size = num_heads // kv_heads
        half_len = tok_local // 2
        score_scale = head_dim ** -0.5
        group_rank = lax.axis_index("cp")
        key_pos = token_positions(groups, tok_local)
        local_idx = jnp.arange(tok_local)
        query_pos = jnp.where(local_idx < half_len, group_rank, 2 * groups - 1 - group_rank) * half_len + local_idx % half_len
        visible = query_pos[:, None] >= key_pos[None, :]
        wq_flat = w_query.reshape(model_width, num_heads * head_dim)
        wk_flat = w_key.reshape(model_width, kv_heads * head_dim)
        wv_flat = w_value.reshape(model_width, kv_heads * head_dim)
        wo_flat = w_out.reshape(num_heads * head_dim, model_width)
        query_heads = jnp.dot(hidden, wq_flat, preferred_element_type=jnp.float32).astype(jnp.bfloat16)
        query_heads = query_heads.reshape(tok_local, kv_heads, group_size, head_dim)
        key_local = jnp.dot(hidden, wk_flat, preferred_element_type=jnp.float32).astype(jnp.bfloat16)
        value_local = jnp.dot(hidden, wv_flat, preferred_element_type=jnp.float32).astype(jnp.bfloat16)
        kv_local = jnp.stack([key_local, value_local]).reshape(2, tok_local, kv_heads, head_dim)
        kv_all = lax.all_gather(kv_local, "cp", axis=1, tiled=True)
        key_rows, value_rows = kv_all[0], kv_all[1]
        scores = jnp.einsum("tkgd,skd->kgts", query_heads, key_rows, preferred_element_type=jnp.float32) * score_scale
        masked = jnp.where(visible, scores, -jnp.inf)
        log_norm = jax.nn.logsumexp(masked, axis=-1)
        att_probs = jnp.exp(masked - log_norm[..., None]).astype(jnp.bfloat16)
        attended = jnp.einsum("kgts,skd->tkgd", att_probs, value_rows, preferred_element_type=jnp.float32).astype(jnp.bfloat16)
        att_flat = attended.reshape(tok_local, num_heads * head_dim)
        output = jnp.dot(att_flat, wo_flat, preferred_element_type=jnp.float32).astype(jnp.bfloat16)
        dout_flat = jnp.einsum("tm,em->te", grad_out, wo_flat, preferred_element_type=jnp.float32).astype(jnp.bfloat16)
        dout_heads = dout_flat.reshape(tok_local, kv_heads, group_size, head_dim)
        delta_rows = jnp.einsum("tkgd,tkgd->kgt", dout_heads, attended, preferred_element_type=jnp.float32)
        d_probs = jnp.einsum("tkgd,skd->kgts", dout_heads, value_rows, preferred_element_type=jnp.float32)
        d_scores = (att_probs.astype(jnp.float32) * (d_probs - delta_rows[..., None])).astype(jnp.bfloat16)
        query_grad = jnp.einsum("kgts,skd->tkgd", d_scores, key_rows, preferred_element_type=jnp.float32) * score_scale
        query_grad = query_grad.astype(jnp.bfloat16).reshape(tok_local, num_heads * head_dim)
        key_part = jnp.einsum("kgts,tkgd->skd", d_scores, query_heads, preferred_element_type=jnp.float32) * score_scale
        value_part = jnp.einsum("kgts,tkgd->skd", att_probs, dout_heads, preferred_element_type=jnp.float32)
        kv_grad = lax.psum_scatter(jnp.stack([key_part, value_part]), "cp", scatter_dimension=1, tiled=True)
        key_grad = kv_grad[0].astype(jnp.bfloat16).reshape(tok_local, kv_heads * head_dim)
        value_grad = kv_grad[1].astype(jnp.bfloat16).reshape(tok_local, kv_heads * head_dim)
        grad_hidden = (
            jnp.einsum("te,me->tm", query_grad, wq_flat, preferred_element_type=jnp.float32)
            + jnp.einsum("te,me->tm", key_grad, wk_flat, preferred_element_type=jnp.float32)
            + jnp.einsum("te,me->tm", value_grad, wv_flat, preferred_element_type=jnp.float32)
        ).astype(jnp.bfloat16)
        weight_parts = (
            jnp.einsum("tm,te->me", hidden, query_grad, preferred_element_type=jnp.float32),
            jnp.einsum("tm,te->me", hidden, key_grad, preferred_element_type=jnp.float32),
            jnp.einsum("tm,te->me", hidden, value_grad, preferred_element_type=jnp.float32),
            jnp.einsum("te,tm->em", att_flat, grad_out, preferred_element_type=jnp.float32),
        )
        grad_w_query, grad_w_key, grad_w_value, grad_w_out = lax.psum(weight_parts, "cp")
        return (
            output,
            grad_hidden,
            grad_w_query.reshape(model_width, num_heads, head_dim),
            grad_w_key.reshape(model_width, kv_heads, head_dim),
            grad_w_value.reshape(model_width, kv_heads, head_dim),
            grad_w_out.reshape(num_heads, head_dim, model_width),
        )

    return jax.shard_map(
        device_layer,
        mesh=mesh,
        in_specs=(row_spec, row_spec, rep_spec, rep_spec, rep_spec, rep_spec),
        out_specs=(row_spec, row_spec, part_spec, part_spec, part_spec, part_spec),
        check_vma=False,
    )
```

profile of v0, /device:TPU:6, one launch (start us, length us, event | category | flops | bytes accessed | tf_op | source)
XLA Modules:
  0.0 1334.4 jit_solution(3829725432202486789)
XLA Ops:
  13.3 4.6 fusion.32
  18.8 6.3 convolution_convert_fusion.1
  26.7 7.6 broadcast_compare_fusion
  34.3 61.6 %all-gather.2.cloned.1.call-done = bf16[2,16384,2,128]{3,1,2,0:T(8,128)(2,1)} async-done(((bf16[2,128,2,128]{3,1,2,0:T(8,128)(2,1)}), bf16[2,16384,2,128]{3,1,2,0:T(8,128)(2,1)}) %all-gather.2.cloned.1.call-update) | async-done | bytes 16777232 | tf_op jit(solution)/shard_map/all_gather | solution.py:43
  95.9 27.1 %fusion.2 = (f32[2,4,128]{2,1,0:T(4,128)S(1)}, f32[2,16384,128,4]{2,1,3,0:T(8,128)}) fusion(pred[128,16384]{0,1:T(8,128)(4,1)S(1)} %broadcast_compare_fusion, bf16[128,2,4,128]{0,3,2,1:T(8,128)(2,1)} %bitcast.165, bf16[2,16384,2,128]{3,1,2,0:T(8,128)(2,1)} %all-gather.2.cloned.1.call-done), kind=kOutput, calls=%fused_computation.6 | convolution fusion | flops 4345297920 | bytes 77860864 | tf_op jit(solution)/shard_map/tkgd,skd->kgts/dot_general | solution.py:45
  122.9 21.3 %exponential_reduce_fusion = f32[2,4,128]{2,1,0:T(4,128)S(1)} fusion(f32[2,16384,128,4]{2,1,3,0:T(8,128)} %get-tuple-element.13, f32[2,4,128]{2,1,0:T(4,128)S(1)} %is-finite_select_fusion, pred[128,16384]{0,1:T(8,128)(4,1)S(1)} %broadcast_compare_fusion), kind=kLoop, calls=%fused_computation.5 | loop fusion | flops 67107840 | bytes 69214208 | tf_op jit(solution)/shard_map/reduce_sum | solution.py:47
  144.2 33.3 %exponential_convert_fusion = bf16[2,4,128,16384]{2,3,1,0:T(8,128)(2,1)} fusion(f32[2,16384,128,4]{2,1,3,0:T(8,128)} %get-tuple-element.13, f32[2,4,128]{2,1,0:T(4,128)S(1)} %log_add_fusion, pred[128,16384]{0,1:T(8,128)(4,1)S(1)} %broadcast_compare_fusion), kind=kLoop, calls=%fused_computation.4 | loop fusion | flops 67108864 | bytes 102764544 | tf_op jit(solution)/shard_map/convert_element_type | solution.py:48
  177.5 22.3 %convolution_bitcast_fusion = f32[1,16384,2,128]{1,3,2,0:T(8,128)} fusion(bf16[128,2,4,128]{0,3,2,1:T(8,128)(2,1)S(1)} %copy.22, bf16[2,4,128,16384]{2,3,1,0:T(8,128)(2,1)} %exponential_convert_fusion), kind=kOutput, calls=%fused_computation.8 | convolution fusion | flops 4294967296 | bytes 50593792 | tf_op jit(solution)/shard_map/kgts,tkgd->skd/dot_general | solution.py:60
  199.9 15.7 %multiply_reduce_fusion = (f32[2,4,128]{2,1,0:T(4,128)S(1)}, bf16[2,128,4,128]{3,1,2,0:T(8,128)(2,1)S(1)}) fusion(f32[2,4,128,128]{2,3,1,0:T(8,128)S(1)} %copy-done.12, bf16[2,4,128,16384]{2,3,1,0:T(8,128)(2,1)} %exponential_convert_fusion, bf16[2,16384,2,128]{3,1,2,0:T(8,128)(2,1)} %all-gather.2.cloned.1.call-done), kind=kOutput, calls=%fused_computation.45 | convolution fusion | flops 4295490560 | bytes 42733568 | tf_op jit(solution)/shard_map/kgts,skd->tkgd/dot_general | solution.py:49
  215.6 25.9 %fusion.1 = bf16[2,4,128,16384]{2,3,1,0:T(8,128)(2,1)} fusion(bf16[2,4,128,16384]{2,3,1,0:T(8,128)(2,1)} %exponential_convert_fusion, bf16[128,2,4,128]{0,3,2,1:T(8,128)(2,1)S(1)} %copy.22, f32[2,4,128]{2,1,0:T(4,128)S(1)} %get-tuple-element.14, bf16[2,16384,2,128]{3,1,2,0:T(8,128)(2,1)} %all-gather.2.cloned.1.call-done), kind=kOutput, calls=%fused_computation.2 | convolution fusion | flops 4362076160 | bytes 75763712 | tf_op jit(solution)/shard_map/tkgd,skd->kgts/dot_general | solution.py:55
  241.5 22.3 %fusion.4 = f32[1,16384,2,128]{1,3,2,0:T(8,128)} fusion(bf16[128,2,4,128]{0,3,2,1:T(8,128)(2,1)S(1)} %bitcast.166, bf16[2,4,128,16384]{2,3,1,0:T(8,128)(2,1)} %fusion.1), kind=kOutput, calls=%fused_computation.11 | convolution fusion | flops 4299161600 | bytes 50593792 | tf_op jit(solution)/shard_map/kgts,tkgd->skd/dot_general | solution.py:59
  263.8 22.5 %pad_maximum_fusion = f32[2,16384,2,128]{1,3,2,0:T(8,128)} fusion(f32[1,16384,2,128]{1,3,2,0:T(8,128)} %convolution_bitcast_fusion, f32[1,16384,2,128]{1,3,2,0:T(8,128)} %fusion.4), kind=kLoop, calls=%fused_computation.7 | loop fusion | flops 8388608 | bytes 67108864 | tf_op jit(solution)/shard_map/stack | solution.py:61
  286.3 15.7 %fusion.35 = bf16[2,128,4,128]{3,1,2,0:T(8,128)(2,1)S(1)} fusion(bf16[2,4,128,16384]{2,3,1,0:T(8,128)(2,1)} %fusion.1, bf16[2,16384,2,128]{3,1,2,0:T(8,128)(2,1)} %all-gather.2.cloned.1.call-done), kind=kOutput, calls=%fused_computation.41 | convolution fusion | flops 4295229440 | bytes 42205184 | tf_op jit(solution)/shard_map/kgts,skd->tkgd/dot_general | solution.py:57
  302.0 8.5 fusion.59
  310.5 17.6 %copy.28 = f32[4096,8,128]{2,1,0:T(8,128)} copy(f32[4096,8,128]{0,2,1:T(8,128)} %bitcast.150) | data formatting | bytes 33554432 | tf_op jit(solution)/shard_map/reshape | solution.py:79
  328.1 8.5 fusion.62
  336.5 626.2 %reduce-scatter.2.cloned.1.call-done = f32[2,128,2,128]{1,3,2,0:T(8,128)} async-done(((f32[2,16384,2,128]{1,3,2,0:T(8,128)}), f32[2,128,2,128]{1,3,2,0:T(8,128)}) %reduce-scatter.2.cloned.1.call-update) | async-done | bytes 262160 | tf_op jit(solution)/shard_map/reduce_scatter | solution.py:61
  966.5 7.2 copy.29
  976.4 7.2 copy.30
  984.5 5.8 convolution_convert_fusion
  992.0 7.3 fusion.20
  999.3 300.3 %all-reduce.3.cloned.1.call-done = (f32[4096,8,128]{2,1,0:T(8,128)}, f32[4096,2,128]{2,1,0:T(2,128)}, f32[4096,2,128]{2,1,0:T(2,128)}, f32[8,128,4096]{2,1,0:T(8,128)}) async-done(((f32[4096,8,128]{2,1,0:T(8,128)}, f32[4096,2,128]{2,1,0:T(2,128)}, f32[4096,2,128]{2,1,0:T(2,128)}, f32[8,128,4096]{2,1,0:T(8,128)}), (f32[4096,8,128]{2,1,0:T(8,128)}, f32[4096,2,128]{2,1,0:T(2,128)}, f32[4096,2,128]{2,1,0:T(2,128)}, ...) | async-done | bytes 41943056 | tf_op jit(solution)/shard_map/psum | solution.py:75
  1299.6 13.2 copy.93
  1321.7 6.2 copy.96
  (64 shorter events, 26.5 us)
Async XLA Ops:
  7.2 1.2 copy-start
  7.2 11.6 copy-start.1
  7.2 88.7 %all-gather.2.cloned.1.call-start = ((), (), s32[]{:S(2)}) async-start(), calls=%async_computation.1 | async-start | bytes 16908288 | tf_op jit(solution)/shard_map/all_gather | solution.py:43
  13.3 949.5 %reduce-scatter.2.cloned.1.call-start = ((), (), s32[]{:S(2)}) async-start(), calls=%async_computation.2 | async-start | bytes 33816576 | tf_op jit(solution)/shard_map/reduce_scatter | solution.py:61
  177.5 22.4 %copy-start.12 = (f32[2,4,128,128]{2,3,1,0:T(8,128)S(1)}, f32[2,4,128,128]{2,3,1,0:T(8,128)}, u32[]{:S(2)}) copy-start(f32[2,4,128,128]{2,3,1,0:T(8,128)} %copy.40) | copy-start | bytes 1572868
  215.5 112.5 %copy-start.7 = (bf16[2,128,4,128]{3,1,2,0:T(8,128)(2,1)}, bf16[2,128,4,128]{3,1,2,0:T(8,128)(2,1)S(1)}, u32[]{:S(2)}) copy-start(bf16[2,128,4,128]{3,1,2,0:T(8,128)(2,1)S(1)} %get-tuple-element.15) | copy-start | bytes 786436
  215.5 25.9 %copy-start.11 = (bf16[128,1024]{0,1:T(8,128)(2,1)S(1)}, bf16[128,1024]{0,1:T(8,128)(2,1)}, u32[]{:S(2)}) copy-start(bf16[128,1024]{0,1:T(8,128)(2,1)} %copy.53) | copy-start | bytes 786436
  286.3 1013.3 %all-reduce.3.cloned.1.call-start = ((), (), s32[]{:S(2)}) async-start(), calls=%async_computation.3 | async-start | bytes 83886080 | tf_op jit(solution)/shard_map/psum | solution.py:75
  302.0 8.5 copy-start.9
  310.5 17.6 %copy-start.2 = (bf16[128,4096]{1,0:T(8,128)(2,1)S(1)}, bf16[128,4096]{1,0:T(8,128)(2,1)}, u32[]{:S(2)}) copy-start(bf16[128,4096]{1,0:T(8,128)(2,1)} %param.7) | copy-start | bytes 3145732
  983.6 0.9 copy-start.8
  983.6 6.7 copy-start.5
  984.5 6.6 copy-start.6
  984.5 7.5 copy-start.10
  1299.6 13.2 copy-start.4
  1299.6 15.3 %copy-start.3 = (f32[4096,2,128]{2,1,0:T(2,128)S(1)}, f32[4096,2,128]{2,1,0:T(2,128)}, u32[]{:S(2)}) copy-start(f32[4096,2,128]{2,1,0:T(2,128)} %get-tuple-element.20) | copy-start | bytes 12582916
  1299.6 18.0 %slice-start = ((s8[16777216]{0:T(1024)(128)(4,1)}), s8[4194304]{0:T(1024)(128)(4,1)S(1)}, s32[]{:S(2)}) async-start(s8[16777216]{0:T(1024)(128)(4,1)} %bitcast.153), calls=%async_computation.4 | async-start | bytes 8388608
  1299.6 19.5 %slice-start.1 = ((s8[16777216]{0:T(1024)(128)(4,1)}), s8[4194304]{0:T(1024)(128)(4,1)S(1)}, s32[]{:S(2)}) async-start(s8[16777216]{0:T(1024)(128)(4,1)} %bitcast.153), calls=%async_computation.5 | async-start | bytes 8388608
  1299.6 20.7 %slice-start.2 = ((s8[16777216]{0:T(1024)(128)(4,1)}), s8[4194304]{0:T(1024)(128)(4,1)S(1)}, s32[]{:S(2)}) async-start(s8[16777216]{0:T(1024)(128)(4,1)} %bitcast.153), calls=%async_computation.6 | async-start | bytes 8388608
  1312.8 8.9 slice-start.3
Sparse Core Ops, SparseCore 0:
  13.4 82.4 all-gather.1
  286.4 676.3 reduce-scatter.1
  983.7 315.8 all-reduce.2
where the time goes:
time: 1340 us; the launch traced here: 1330 us
  waiting for transfers between devices  988 us (74%)
  matrix products  181 us (14%)
  other arithmetic  85.4 us (6%)
  local copies, waits for them, and re-layouts  65.7 us (5%)
  between operations  14 us (1%)
    reduce_scatter x1, waiting for transfers between devices, device_layer(): lax.psum_scatter(jnp.stack([key_part, value_part]), 'cp', scatter_dimensi...  626 us
    psum x1, waiting for transfers between devices, device_layer(): lax.psum(weight_parts, 'cp')  300 us
    all_gather x1, waiting for transfers between devices, device_layer(): kv_all = lax.all_gather(kv_local, 'cp', axis=1, tiled=True)  61.6 us
    convert_element_type x1, other arithmetic, device_layer(): att_probs = jnp.exp(masked - log_norm[..., None]).astype(jnp.bfloat16)  33.3 us
    unnamed x39, local copies, waits for them, and re-layouts  31.4 us
    dot_general x1, matrix products, device_layer(): jnp.einsum('tkgd,skd->kgts', query_heads, key_rows, preferred_element_typ...  27.1 us
  transfers between devices with their start and end apart: 3, of which 3 were waited for; matrix products, arithmetic and copies ran while one was open for 6% of the time, Pallas kernels for 0%

commit v1 on v0

v1 whole, which is shorter than its diff:
```python
import functools
import math

import jax
import jax.numpy as jnp
from jax import lax
from jax.experimental import pallas as pl
from jax.experimental.layout import Layout, with_layout_constraint
from jax.experimental.pallas import tpu as pltpu
from jax.sharding import PartitionSpec as P

F32, BF16 = jnp.float32, jnp.bfloat16
DEVS_PER_TILE = 8
PLANES = 4
NT = (((1,), (1,)), ((), ()))
TN = (((0,), (0,)), ((), ()))
NN = (((1,), (0,)), ((), ()))


def dot(a, b, dims):
    return lax.dot_general(a, b, dims, preferred_element_type=F32)


def stack_heads(ref, half_len, group, head_dim):
    parts = []
    for half in (1, 0):
        for g in range(group):
            parts.append(ref[half * half_len:(half + 1) * half_len, g * head_dim:(g + 1) * head_dim])
    return jnp.concatenate(parts, axis=0)


def unstack_heads(ref, rows, half_len, group, head_dim):
    for i, half in enumerate((1, 0)):
        for g in range(group):
            block = rows[(i * group + g) * half_len:(i * group + g + 1) * half_len]
            ref[half * half_len:(half + 1) * half_len, g * head_dim:(g + 1) * head_dim] = block


def place(tile, per, plane, layer):
    return pl.ds(tile * per % plane, per), jnp.bitwise_xor(tile * per // plane, layer)


def tile_mask(tile, half, rank, half_len, keys, cols):
    key_dev = tile * (keys // half_len) + lax.broadcasted_iota(jnp.int32, (keys, cols), 0) // half_len
    key_off = lax.broadcasted_iota(jnp.int32, (keys, cols), 0) % half_len
    q_off = lax.broadcasted_iota(jnp.int32, (keys, cols), 1) % half_len
    sign = 1 if half == 0 else -1
    return sign * (rank - key_dev) * half_len + q_off - key_off >= 0


def ranks_of(devs, plane):
    me = lax.axis_index("cp")
    layer = me // plane
    mirror = (PLANES - 1 - layer) * plane + me % plane
    return layer, jnp.where(pl.program_id(0) == 0, me, mirror)


def fwd_kernel(devs, half_len, group, head_dim, scale2, q_ref, kv_ref, do_ref, o_ref, stats_ref, qs, m_ref, l_ref, acc):
    plane = devs // PLANES
    layer, rank = ranks_of(devs, plane)
    per = min(DEVS_PER_TILE, plane)
    tiles = devs // per
    diag = rank // per
    nq = group * half_len
    keys = per * half_len
    k_cols, v_cols = pl.ds(0, head_dim), pl.ds(head_dim, head_dim)
    qs[...] = stack_heads(q_ref, half_len, group, head_dim)

    def update(k, v, cols, mask, first=False):
        s = dot(k, qs[cols, :], NT) * scale2
        if mask is not None:
            s = jnp.where(mask, s, -jnp.inf)
        top = jnp.max(s, axis=0, keepdims=True)
        if not first:
            old = m_ref[:, cols]
            top = jnp.maximum(old, top)
            shrink = jnp.exp2(old - top)
        p = jnp.exp2(s - top)
        total = jnp.sum(p, axis=0, keepdims=True)
        out = dot(v, p.astype(BF16), TN)
        if not first:
            total = total + l_ref[:, cols] * shrink
            out = out + acc[:, cols] * shrink
        m_ref[:, cols] = top
        l_ref[:, cols] = total
        acc[:, cols] = out

    high, low, every = pl.ds(0, nq), pl.ds(nq, nq), pl.ds(0, 2 * nq)

    def part(kind, tile, half):
        return kv_ref[(*place(tile, per, plane, layer), half, slice(None), kind)].reshape(keys, head_dim)

    def both(kind, tile):
        return kv_ref[(*place(tile, per, plane, layer), slice(None), slice(None), kind)].reshape(2 * keys, head_dim)

    update(part(k_cols, diag, 0), part(v_cols, diag, 0), low, tile_mask(diag, 0, rank, half_len, keys, nq), first=True)
    update(part(k_cols, diag, 0), part(v_cols, diag, 0), high, None, first=True)
    update(part(k_cols, diag, 1), part(v_cols, diag, 1), high, tile_mask(diag, 1, rank, half_len, keys, nq))

    @pl.loop(0, diag)
    def _(t):
        update(part(k_cols, t, 0), part(v_cols, t, 0), every, None)

    @pl.loop(diag + 1, tiles)
    def _(t):
        update(both(k_cols, t), both(v_cols, t), high, None)

    out_t = acc[...] / l_ref[...]
    out = jnp.transpose(out_t).astype(BF16)
    unstack_heads(o_ref, out, half_len, group, head_dim)
    do_t = jnp.transpose(stack_heads(do_ref, half_len, group, head_dim).astype(F32))
    delta = jnp.sum(do_t * out_t.astype(BF16).astype(F32), axis=0, keepdims=True)
    stats_ref[0, 0:1, :] = m_ref[...] + jnp.log2(l_ref[...])
    stats_ref[0, 1:2, :] = delta


def bwd_kernel(devs, half_len, group, head_dim, scale, scale2, q_ref, kv_ref, do_ref, stats_ref,
               dq_ref, dkv_ref, qs, dos, dq_acc):
    plane = devs // PLANES
    layer, rank = ranks_of(devs, plane)
    per = min(DEVS_PER_TILE, plane)
    tiles = devs // per
    diag = rank // per
    nq = group * half_len
    keys = per * half_len
    k_cols, v_cols = pl.ds(0, head_dim), pl.ds(head_dim, head_dim)
    qs[...] = stack_heads(q_ref, half_len, group, head_dim)
    dos[...] = stack_heads(do_ref, half_len, group, head_dim)
    high, every = pl.ds(0, nq), pl.ds(0, 2 * nq)

    def grads(k, v, cols, mask, first=False):
        q, do = qs[cols, :], dos[cols, :]
        s = dot(k, q, NT) * scale2 - stats_ref[0, 0:1, cols]
        if mask is not None:
            s = jnp.where(mask, s, -jnp.inf)
        p = jnp.exp2(s).astype(BF16)
        dv = dot(p, do, NN)
        dp = dot(v, do, NT) - stats_ref[0, 1:2, cols]
        ds = (p.astype(F32) * dp).astype(BF16)
        dk = dot(ds, q, NN) * scale
        dq = dot(k, ds, TN)
        dq_acc[:, cols] = dq if first else dq_acc[:, cols] + dq
        return dk, dv

    def part(kind, tile, half):
        return kv_ref[(*place(tile, per, plane, layer), half, slice(None), kind)].reshape(keys, head_dim)

    def put(tile, half, dk, dv):
        for kind, value in enumerate((dk, dv)):
            where = (*place(tile, per, plane, layer), kind, half)
            dkv_ref[where] = dkv_ref[where] + value.reshape(per, half_len, head_dim)

    @pl.when(pl.program_id(0) == 0)
    def _():
        @pl.loop(0, plane)
        def _(j):
            dkv_ref[j] = jnp.zeros_like(dkv_ref[j])

    mask = jnp.concatenate(
        [jnp.ones((keys, nq), jnp.bool_), tile_mask(diag, 0, rank, half_len, keys, nq)], axis=1)
    dk, dv = grads(part(k_cols, diag, 0), part(v_cols, diag, 0), every, mask, first=True)
    put(diag, 0, dk, dv)
    dk, dv = grads(part(k_cols, diag, 1), part(v_cols, diag, 1), high, tile_mask(diag, 1, rank, half_len, keys, nq))
    put(diag, 1, dk, dv)

    @pl.loop(0, diag)
    def _(t):
        dk, dv = grads(part(k_cols, t, 0), part(v_cols, t, 0), every, None)
        put(t, 0, dk, dv)

    @pl.loop(diag + 1, tiles)
    def _(t):
        where = (*place(t, per, plane, layer), slice(None), slice(None))
        k = kv_ref[(*where, k_cols)].reshape(2 * keys, head_dim)
        v = kv_ref[(*where, v_cols)].reshape(2 * keys, head_dim)
        dk, dv = grads(k, v, high, None)
        dk = dk.reshape(per, 2, half_len, head_dim)
        dv = dv.reshape(per, 2, half_len, head_dim)
        for half in range(2):
            put(t, half, dk[:, half], dv[:, half])

    unstack_heads(dq_ref, jnp.transpose(dq_acc[...] * scale).astype(BF16), half_len, group, head_dim)


def attention_calls(devs, tok, group, head_dim):
    half_len = tok // 2
    plane = devs // PLANES
    scale = head_dim ** -0.5
    scale2 = scale * math.log2(math.e)
    rows = 2 * group * half_len
    wide = group * head_dim
    row_spec = pl.BlockSpec((None, tok, wide), lambda h: (h, 0, 0))
    kv_spec = pl.BlockSpec((plane, PLANES, 2, half_len, 2 * head_dim), lambda h: (0, 0, 0, 0, 0))
    stats_spec = pl.BlockSpec((1, 8, rows), lambda h: (h, 0, 0))
    pairs = 2 * group * half_len * half_len * (2 * devs + 1)
    params = pltpu.CompilerParams(dimension_semantics=("arbitrary",), vmem_limit_bytes=62 * 1024 * 1024)
    kv_bytes = devs * tok * 2 * head_dim * 2
    row_shape = jax.ShapeDtypeStruct((2, tok, wide), BF16)
    forward = pl.pallas_call(
        functools.partial(fwd_kernel, devs, half_len, group, head_dim, scale2),
        grid=(2,),
        in_specs=[row_spec, kv_spec, row_spec],
        out_specs=[row_spec, stats_spec],
        out_shape=[row_shape, jax.ShapeDtypeStruct((2, 8, rows), F32)],
        scratch_shapes=[pltpu.VMEM((rows, head_dim), BF16), pltpu.VMEM((1, rows), F32), pltpu.VMEM((1, rows), F32),
                        pltpu.VMEM((head_dim, rows), F32)],
        compiler_params=params,
        cost_estimate=pl.CostEstimate(flops=pairs * 4 * head_dim, bytes_accessed=kv_bytes, transcendentals=pairs),
        name="attention_forward",
    )
    part_shape = (plane, PLANES, 2, 2, half_len, head_dim)
    backward = pl.pallas_call(
        functools.partial(bwd_kernel, devs, half_len, group, head_dim, scale, scale2),
        grid=(2,),
        in_specs=[row_spec, kv_spec, row_spec, stats_spec],
        out_specs=[row_spec, pl.BlockSpec(part_shape, lambda h: (0,) * 6)],
        out_shape=[row_shape, jax.ShapeDtypeStruct(part_shape, F32)],
        scratch_shapes=[pltpu.VMEM((rows, head_dim), BF16), pltpu.VMEM((rows, head_dim), BF16),
                        pltpu.VMEM((head_dim, rows), F32)],
        compiler_params=params,
        cost_estimate=pl.CostEstimate(flops=pairs * 10 * head_dim, bytes_accessed=3 * kv_bytes, transcendentals=pairs),
        name="attention_backward",
    )
    return forward, backward


def weight_grads_kernel(count, heads, head_dim, x_ref, *refs):
    for g_ref, out_ref in zip(refs[:count], refs[count:]):
        grad = dot(x_ref[...], g_ref[...], TN)
        for h in range(heads):
            out_ref[:, h, :] = grad[:, h * head_dim:(h + 1) * head_dim]


def weight_grads(x, gs, heads):
    tok, width = x.shape
    head_dim = gs[0].shape[1] // heads
    block = min(512, width)
    return pl.pallas_call(
        functools.partial(weight_grads_kernel, len(gs), heads, head_dim),
        grid=(width // block,),
        in_specs=[pl.BlockSpec((tok, block), lambda i: (0, i))] + [pl.BlockSpec(g.shape, lambda i: (0, 0)) for g in gs],
        out_specs=[pl.BlockSpec((block, heads, head_dim), lambda i: (i, 0, 0)) for _ in gs],
        out_shape=[jax.ShapeDtypeStruct((width, heads, head_dim), F32) for _ in gs],
        compiler_params=pltpu.CompilerParams(dimension_semantics=("arbitrary",)),
        cost_estimate=pl.CostEstimate(flops=2 * tok * width * heads * head_dim * len(gs),
                                      bytes_accessed=4 * width * heads * head_dim * len(gs), transcendentals=0),
        name="weight_grads",
    )(x, *gs)


def solution(mesh):
    devs = mesh.shape["cp"]
    row_spec = P(("dp", "cp"), None)
    rep_spec = P(None, None, None)
    part_spec = P("dp", None, None)
    plane = devs // PLANES
    plane_groups = [[z * plane + i for i in range(plane)] for z in range(PLANES)]

    def to_plane(value, step):
        return lax.ppermute(value, "cp", [(i, (i // plane ^ step) * plane + i % plane) for i in range(devs)])

    def device_layer(hidden, grad_out, w_query, w_key, w_value, w_out):
        tok, width = hidden.shape
        heads, head_dim = w_query.shape[1:]
        kv_heads = w_key.shape[1]
        group = heads // kv_heads
        wide = group * head_dim
        forward, backward = attention_calls(devs, tok, group, head_dim)
        wq = w_query.reshape(width, heads * head_dim)
        wk = w_key.reshape(width, kv_heads * head_dim)
        wv = w_value.reshape(width, kv_heads * head_dim)
        wo = w_out.reshape(heads * head_dim, width)
        upper = lax.axis_index("cp") // plane >= PLANES // 2

        def mine_and_other(rows):
            first, second = jnp.split(rows, 2, axis=1)
            return jnp.where(upper, second, first), jnp.where(upper, first, second)

        def in_head_order(mine, other):
            return jnp.concatenate([jnp.where(upper, other, mine), jnp.where(upper, mine, other)], axis=1)

        key_mine, key_other = mine_and_other(dot(hidden, wk, NN).astype(BF16))
        value_mine, value_other = mine_and_other(dot(hidden, wv, NN).astype(BF16))
        kv_mine = jnp.concatenate([key_mine, value_mine], axis=1)
        kv_other = to_plane(jnp.concatenate([key_other, value_other], axis=1), PLANES - 1)
        near = jnp.concatenate([kv_mine, kv_other], axis=0)
        far = to_plane(near, 1)
        kv_local = jnp.concatenate([kv_mine, far, kv_other], axis=0)
        kv_local = with_layout_constraint(kv_local, Layout(major_to_minor=(0, 1)))
        kv_all = lax.all_gather(kv_local, "cp", axis=0, tiled=True, axis_index_groups=plane_groups)
        kv_all = with_layout_constraint(kv_all, Layout(major_to_minor=(0, 1)))
        kv_blocks = kv_all.reshape(plane, PLANES, 2, tok // 2, 2 * head_dim)

        query_mine, query_other = mine_and_other(dot(hidden, wq, NN).astype(BF16))
        dout_mine, dout_other = mine_and_other(dot(grad_out, wo, NT).astype(BF16))
        query = jnp.stack([query_mine, to_plane(query_other, PLANES - 1)])
        dout = jnp.stack([dout_mine, to_plane(dout_other, PLANES - 1)])
        att_parts, stats = forward(query, kv_blocks, dout)
        dq_parts, kv_part = backward(query, kv_blocks, dout, stats)

        slot_rows = 2 * tok
        kv_part = kv_part.reshape(plane * PLANES * slot_rows, head_dim)
        kv_part = lax.psum_scatter(kv_part, "cp", scatter_dimension=0, tiled=True, axis_index_groups=plane_groups)
        attended = in_head_order(att_parts[0], to_plane(att_parts[1], PLANES - 1))
        query_grad = in_head_order(dq_parts[0], to_plane(dq_parts[1], PLANES - 1))
        out_part = dot(attended, grad_out, TN).reshape(heads, head_dim, width)
        query_part, = weight_grads(hidden, [query_grad], heads)
        output = jnp.dot(attended, wo, preferred_element_type=F32).astype(BF16)
        hidden_part = dot(query_grad, wq, NT)
        kv_part, out_part, query_part, output, hidden_part = lax.optimization_barrier(
            (kv_part, out_part, query_part, output, hidden_part))

        slots = kv_part.reshape(PLANES, slot_rows, head_dim)
        mine = slots[0] + to_plane(slots[1], 1)
        other = to_plane(slots[2], 2) + to_plane(slots[3], 3)
        kv_grad = in_head_order(mine, other).astype(BF16)
        key_grad, value_grad = kv_grad[:tok], kv_grad[tok:]
        key_part, value_part = weight_grads(hidden, [key_grad, value_grad], kv_heads)
        grads = lax.psum((query_part, key_part, value_part, out_part), "cp")
        grad_hidden = (hidden_part + dot(key_grad, wk, NT) + dot(value_grad, wv, NT)).astype(BF16)
        return (output, grad_hidden, *grads)

    return jax.shard_map(
        device_layer,
        mesh=mesh,
        in_specs=(row_spec, row_spec, rep_spec, rep_spec, rep_spec, rep_spec),
        out_specs=(row_spec, row_spec, part_spec, part_spec, part_spec, part_spec),
        check_vma=False,
    )
```

time: 1340 us -> 616 us (0.46)
  waiting for transfers between devices: 988 us -> 418 us
  matrix products: 181 us -> 41.5 us
  Pallas kernels: 0 us -> 89.3 us
  other arithmetic: 85.4 us -> 4.66 us
  local copies, waits for them, and re-layouts: 65.7 us -> 31.9 us
  starting transfers between devices: 0.12 us -> 15.8 us
    reduce_scatter x1, waiting for transfers between devices: 626 us -> 71.2 us  [device_layer(): lax.psum_scatter(kv_part, 'cp', scatter_dimension=0, tiled=True, axis_ind...]
    dot_general x18 -> x9, matrix products: 181 us -> 41.5 us  [the longest x8 35.9 us: dot(): return lax.dot_general(a, b, dims, preferred_element_type=F32)]
    pallas_call x0 -> x4, Pallas kernels: none -> 89.3 us  [the longest x1 39 us: device_layer(): dq_parts, kv_part = backward(query, kv_blocks, dout, stats)]
    convert_element_type x1 -> x0, other arithmetic: 33.3 us -> none  [device_layer(): att_probs = jnp.exp(masked - log_norm[..., None]).astype(jnp.bfloat16)]
    reshape x6 -> x0, local copies, waits for them, and re-layouts: 33.2 us -> none  [the longest x1 17.6 us: device_layer(): grad_w_query.reshape(model_width, num_heads, head_dim)]
    all_gather x1, waiting for transfers between devices: 61.6 us -> 32.6 us  [device_layer(): lax.all_gather(kv_local, 'cp', axis=0, tiled=True, axis_index_groups=plan...]
    ppermute x0 -> x9, waiting for transfers between devices: none -> 21.8 us  [to_plane(): lax.ppermute(value, 'cp', [(i, (i // plane ^ step) * plane + i % plane) f...]
    reduce_sum x1 -> x0, other arithmetic: 21.3 us -> none  [device_layer(): log_norm = jax.nn.logsumexp(masked, axis=-1)]
  transfers between devices with their start and end apart: 3 -> 12, of which waited for: 3 -> 10; matrix products, arithmetic and copies ran while one was open for 6% -> 6% of each run, Pallas kernels for 0% -> 2%
where the time goes in v1:
time: 616 us; the launch traced here: 615 us
  waiting for transfers between devices  418 us (68%)
  Pallas kernels  89.3 us (14%)
  matrix products  41.5 us (7%)
  local copies, waits for them, and re-layouts  31.9 us (5%)
  starting transfers between devices  15.8 us (3%)
  between operations  13.9 us (2%)
    psum x1, waiting for transfers between devices, device_layer(): grads = lax.psum((query_part, key_part, value_part, out_part), 'cp')  293 us
    reduce_scatter x1, waiting for transfers between devices, device_layer(): lax.psum_scatter(kv_part, 'cp', scatter_dimension=0, tiled=True, axis_ind...  71.2 us
    pallas_call x1, Pallas kernels, device_layer(): dq_parts, kv_part = backward(query, kv_blocks, dout, stats)  39 us
    dot_general x8, matrix products, dot(): return lax.dot_general(a, b, dims, preferred_element_type=F32)  35.9 us
    all_gather x1, waiting for transfers between devices, device_layer(): lax.all_gather(kv_local, 'cp', axis=0, tiled=True, axis_index_groups=plan...  32.6 us
    unnamed x34, local copies, waits for them, and re-layouts  30.8 us
    pallas_call x1, Pallas kernels, device_layer(): att_parts, stats = forward(query, kv_blocks, dout)  28 us
    pallas_call x2, Pallas kernels, weight_grads(): pl.pallas_call(functools.partial(weight_grads_kernel, len(gs), heads, hea...  22.3 us
  transfers between devices with their start and end apart: 12, of which 10 were waited for; matrix products, arithmetic and copies ran while one was open for 6% of the time, Pallas kernels for 2%

profile of v1, /device:TPU:6, one launch (start us, length us, event | category | flops | bytes accessed | tf_op | source)
XLA Modules:
  0.0 615.5 jit_solution(4030855529772230575)
XLA Ops:
  7.2 2.5 fusion.20
  9.7 2.4 fusion.23
  12.2 4.1 collective-permute-start.1
  18.7 5.0 collective-permute-done.2
  24.4 4.6 fusion.17
  29.1 3.3 collective-permute-start
  32.4 6.3 %convolution_convert_fusion.1 = bf16[128,1024]{1,0:T(8,128)(2,1)S(1)} fusion(bf16[128,4096]{1,0:T(8,128)(2,1)S(1)} %copy-done, bf16[1024,4096]{1,0:T(8,128)(2,1)} %bitcast.54), kind=kOutput, calls=%fused_computation.21 | convolution fusion | flops 1073872896 | bytes 9699328 | tf_op jit(solution)/shard_map/dot_general | solution.py:21
  39.5 5.4 collective-permute-done.3
  45.7 32.6 %all-gather.2.cloned.1.call-done = bf16[16384,256]{1,0:T(8,128)(2,1)} async-done(((bf16[512,256]{1,0:T(8,128)(2,1)}), bf16[16384,256]{1,0:T(8,128)(2,1)}) %all-gather.2.cloned.1.call-update) | async-done | bytes 8388624 | tf_op jit(solution)/shard_map/all_gather | solution.py:290
  78.3 28.0 %attention_forward.1 = (bf16[2,128,512]{2,1,0:T(8,128)(2,1)}, f32[2,8,512]{2,1,0:T(8,128)}) custom-call(bf16[2,128,512]{2,1,0:T(8,128)(2,1)} %pad_maximum_fusion.q_ref, bf16[32,4,2,64,256]{4,3,2,1,0:T(8,128)(2,1)} %bitcast.67, bf16[2,128,512]{2,1,0:T(8,128)(2,1)} %pad_maximum_fusion.2.do_ref), custom_call_target="tpu_custom_call" | custom-call | flops 4311744512 | bytes 8388608 | tf_op jit(solution)/shard_map/attention_forward/pallas_call | solution.py:298
  106.3 39.0 %attention_backward.1 = (bf16[2,128,512]{2,1,0:T(8,128)(2,1)}, f32[32,4,2,2,64,128]{5,4,3,2,1,0:T(8,128)}) custom-call(bf16[2,128,512]{2,1,0:T(8,128)(2,1)} %pad_maximum_fusion.q_ref, bf16[32,4,2,64,256]{4,3,2,1,0:T(8,128)(2,1)} %bitcast.68, bf16[2,128,512]{2,1,0:T(8,128)(2,1)} %pad_maximum_fusion.2.do_ref, f32[2,8,512]{2,1,0:T(8,128)} %get-tuple-element.17.stats_ref), custom_call_target="tpu_custom_call" | custom-call | flops 10779361280 | bytes 25165824 | tf_op jit(solution)/shard_map/attention_backward/pallas_call | solution.py:299
  146.2 3.1 collective-permute-start.5
  149.8 3.4 collective-permute-done.5
  154.0 13.2 %weight_grads.2 = f32[4096,8,128]{2,1,0:T(8,128)} custom-call(bf16[128,4096]{1,0:T(8,128)(2,1)} %x_ref.3, bf16[128,1024]{1,0:T(8,128)(2,1)} %pad_maximum_fusion.4.refs_0_), custom_call_target="tpu_custom_call" | custom-call | flops 1073741824 | bytes 16777216 | tf_op jit(solution)/shard_map/weight_grads/pallas_call | solution.py:238
  167.2 5.6 convolution_convert_fusion
  172.8 7.6 %fusion = f32[128,4096]{1,0:T(8,128)} fusion(bf16[512,8,8,128]{3,2,1,0:T(8,128)(2,1)} %bitcast.66, bf16[128,512]{1,0:T(8,128)(2,1)S(1)} %get-tuple-element.38, bf16[128,512]{1,0:T(8,128)(2,1)S(1)} %get-tuple-element.37), kind=kOutput, calls=%fused_computation | convolution fusion | flops 1074266112 | bytes 10747904 | tf_op jit(solution)/shard_map/dot_general | solution.py:21
  180.4 8.1 %fusion.26 = f32[1024,4096]{1,0:T(8,128)} fusion(bf16[128,4096]{1,0:T(8,128)(2,1)S(1)} %copy-done, bf16[128,512]{1,0:T(8,128)(2,1)S(1)} %get-tuple-element.40, bf16[128,512]{1,0:T(8,128)(2,1)S(1)} %get-tuple-element.39), kind=kOutput, calls=%fused_computation.29 | convolution fusion | flops 1074266112 | bytes 18087936 | tf_op jit(solution)/shard_map/dot_general | solution.py:21
  188.6 71.2 %reduce-scatter.2.cloned.1.call-done = f32[1024,128]{1,0:T(8,128)} async-done(((f32[32768,128]{1,0:T(8,128)}), f32[1024,128]{1,0:T(8,128)}) %reduce-scatter.2.cloned.1.call-update) | async-done | bytes 524304 | tf_op jit(solution)/shard_map/reduce_scatter | solution.py:303
  272.7 9.2 %weight_grads.3 = (f32[4096,2,128]{2,1,0:T(2,128)}, f32[4096,2,128]{2,1,0:T(2,128)}) custom-call(bf16[128,4096]{1,0:T(8,128)(2,1)} %x_ref.3, bf16[128,256]{1,0:T(8,128)(2,1)} %get-tuple-element.46.refs_0_, bf16[128,256]{1,0:T(8,128)(2,1)} %get-tuple-element.45.refs_1_), custom_call_target="tpu_custom_call" | custom-call | flops 536870912 | bytes 8388608 | tf_op jit(solution)/shard_map/weight_grads/pallas_call | solution.py:238
  283.5 2.6 convolution_add_fusion.1
  287.9 292.7 %all-reduce.3.cloned.1.call-done = (f32[4096,8,128]{2,1,0:T(8,128)}, f32[4096,2,128]{2,1,0:T(2,128)}, f32[4096,2,128]{2,1,0:T(2,128)}, f32[8,128,4096]{2,1,0:T(8,128)}) async-done(((f32[4096,8,128]{2,1,0:T(8,128)}, f32[4096,2,128]{2,1,0:T(2,128)}, f32[4096,2,128]{2,1,0:T(2,128)}, f32[8,128,4096]{2,1,0:T(8,128)}), (f32[4096,8,128]{2,1,0:T(8,128)}, f32[4096,2,128]{2,1,0:T(2,128)}, f32[4096,2,128]{2,1,0:T(2,128)}, ...) | async-done | bytes 41943056 | tf_op jit(solution)/shard_map/psum | solution.py:319
  580.6 13.2 %copy.49 = f32[4096,8,128]{2,1,0:T(8,128)} copy(f32[4096,8,128]{2,1,0:T(8,128)} %get-tuple-element.55) | data formatting | bytes 33554432
  595.9 2.5 copy-done.2
  602.8 6.2 %copy.52 = f32[8,128,4096]{2,1,0:T(8,128)} copy(f32[8,128,4096]{2,1,0:T(8,128)S(1)} %bitcast.58) | data formatting | bytes 33554432
  (67 shorter events, 29.9 us)
Async XLA Ops:
  7.2 25.2 %copy-start = (bf16[128,4096]{1,0:T(8,128)(2,1)S(1)}, bf16[128,4096]{1,0:T(8,128)(2,1)}, u32[]{:S(2)}) copy-start(bf16[128,4096]{1,0:T(8,128)(2,1)} %param.7) | copy-start | bytes 3145732
  7.2 71.1 %all-gather.2.cloned.1.call-start = ((), (), s32[]{:S(2)}) async-start(), calls=%async_computation.1 | async-start | bytes 8650752 | tf_op jit(solution)/shard_map/all_gather | solution.py:290
  7.2 17.2 %copy-start.6 = (bf16[128,4096]{1,0:T(8,128)(2,1)S(1)}, bf16[128,4096]{1,0:T(8,128)(2,1)}, u32[]{:S(2)}) copy-start(bf16[128,4096]{1,0:T(8,128)(2,1)} %x_ref.3) | copy-start | bytes 3145732
  12.2 6.4 %collective-permute-start.1 = (bf16[128,256]{1,0:T(8,128)(2,1)S(1)}, bf16[128,256]{1,0:T(8,128)(2,1)S(1)}, u32[]{:S(2)}, u32[]{:S(2)}) collective-permute-start(bf16[128,256]{1,0:T(8,128)(2,1)S(1)} %pad_maximum_fusion.9), channel_id=1, source_target_pairs={{0,96},{1,97},{2,98},{3,99},{4,100},{5,101},{6,102},{7,103},{8,104... | collective-permute-start | bytes 196616 | tf_op jit(solution)/shard_map/ppermute | solution.py:260
  18.6 5.0 collective-permute-start.2
  24.4 235.4 %reduce-scatter.2.cloned.1.call-start = ((), (), s32[]{:S(2)}) async-start(), calls=%async_computation.2 | async-start | bytes 17301504 | tf_op jit(solution)/shard_map/reduce_scatter | solution.py:303
  29.1 9.7 %collective-permute-start = (bf16[128,512]{1,0:T(8,128)(2,1)S(1)}, bf16[128,512]{1,0:T(8,128)(2,1)S(1)}, u32[]{:S(2)}, u32[]{:S(2)}) collective-permute-start(bf16[128,512]{1,0:T(8,128)(2,1)S(1)} %get-tuple-element.44), channel_id=1, source_target_pairs={{0,96},{1,97},{2,98},{3,99},{4,100},{5,101},{6,102},{7,103},{8,104... | collective-permute-start | bytes 393224 | tf_op jit(solution)/shard_map/ppermute | solution.py:260
  38.7 6.3 %collective-permute-start.3 = (bf16[128,512]{1,0:T(8,128)(2,1)S(1)}, bf16[128,512]{1,0:T(8,128)(2,1)S(1)}, u32[]{:S(2)}, u32[]{:S(2)}) collective-permute-start(bf16[128,512]{1,0:T(8,128)(2,1)S(1)} %get-tuple-element.42), channel_id=1, source_target_pairs={{0,96},{1,97},{2,98},{3,99},{4,100},{5,101},{6,102},{7,103},{8,104... | collective-permute-start | bytes 393224 | tf_op jit(solution)/shard_map/ppermute | solution.py:260
  145.3 4.0 copy-start.8
  145.3 435.3 %all-reduce.3.cloned.1.call-start = ((), (), s32[]{:S(2)}) async-start(), calls=%async_computation.3 | async-start | bytes 83886080 | tf_op jit(solution)/shard_map/psum | solution.py:319
  146.2 7.0 %collective-permute-start.5 = (bf16[128,512]{1,0:T(8,128)(2,1)S(1)}, bf16[128,512]{1,0:T(8,128)(2,1)S(1)}, u32[]{:S(2)}, u32[]{:S(2)}) collective-permute-start(bf16[128,512]{1,0:T(8,128)(2,1)S(1)} %slice_bitcast_fusion), channel_id=1, source_target_pairs={{0,96},{1,97},{2,98},{3,99},{4,100},{5,101},{6,102},{7,103},{8,104... | collective-permute-start | bytes 393224 | tf_op jit(solution)/shard_map/ppermute | solution.py:260
  149.3 17.8 %collective-permute-start.4 = (bf16[128,512]{1,0:T(8,128)(2,1)S(1)}, bf16[128,512]{1,0:T(8,128)(2,1)S(1)}, u32[]{:S(2)}, u32[]{:S(2)}) collective-permute-start(bf16[128,512]{1,0:T(8,128)(2,1)S(1)} %slice_bitcast_fusion.1), channel_id=1, source_target_pairs={{0,96},{1,97},{2,98},{3,99},{4,100},{5,101},{6,102},{7,103},{8,104... | collective-permute-start | bytes 393224 | tf_op jit(solution)/shard_map/ppermute | solution.py:260
  260.9 6.3 %collective-permute-start.8 = (f32[256,128]{1,0:T(8,128)S(1)}, f32[256,128]{1,0:T(8,128)S(1)}, u32[]{:S(2)}, u32[]{:S(2)}) collective-permute-start(f32[256,128]{1,0:T(8,128)S(1)} %get-tuple-element.34), channel_id=1, source_target_pairs={{0,32},{1,33},{2,34},{3,35},{4,36},{5,37},{6,38},{7,39},{8,40},{9,... | collective-permute-start | bytes 393224 | tf_op jit(solution)/shard_map/ppermute | solution.py:260
  262.5 6.9 %collective-permute-start.7 = (f32[256,128]{1,0:T(8,128)S(1)}, f32[256,128]{1,0:T(8,128)S(1)}, u32[]{:S(2)}, u32[]{:S(2)}) collective-permute-start(f32[256,128]{1,0:T(8,128)S(1)} %get-tuple-element.35), channel_id=1, source_target_pairs={{0,96},{1,97},{2,98},{3,99},{4,100},{5,101},{6,102},{7,103},{8,104... | collective-permute-start | bytes 393224 | tf_op jit(solution)/shard_map/ppermute | solution.py:260
  264.7 6.5 %collective-permute-start.6 = (f32[256,128]{1,0:T(8,128)S(1)}, f32[256,128]{1,0:T(8,128)S(1)}, u32[]{:S(2)}, u32[]{:S(2)}) collective-permute-start(f32[256,128]{1,0:T(8,128)S(1)} %get-tuple-element.36), channel_id=1, source_target_pairs={{0,64},{1,65},{2,66},{3,67},{4,68},{5,69},{6,70},{7,71},{8,72},{9,... | collective-permute-start | bytes 393224 | tf_op jit(solution)/shard_map/ppermute | solution.py:260
  283.5 2.6 copy-start.5
  283.5 2.6 copy-start.10
  580.6 13.2 %copy-start.3 = (f32[4096,2,128]{2,1,0:T(2,128)S(1)}, f32[4096,2,128]{2,1,0:T(2,128)}, u32[]{:S(2)}) copy-start(f32[4096,2,128]{2,1,0:T(2,128)} %get-tuple-element.56) | copy-start | bytes 12582916
  580.6 19.9 %slice-start = ((s8[16777216]{0:T(1024)(128)(4,1)}), s8[4194304]{0:T(1024)(128)(4,1)S(1)}, s32[]{:S(2)}) async-start(s8[16777216]{0:T(1024)(128)(4,1)} %bitcast.57), calls=%async_computation.4 | async-start | bytes 8388608
  580.6 19.9 %slice-start.1 = ((s8[16777216]{0:T(1024)(128)(4,1)}), s8[4194304]{0:T(1024)(128)(4,1)S(1)}, s32[]{:S(2)}) async-start(s8[16777216]{0:T(1024)(128)(4,1)} %bitcast.57), calls=%async_computation.5 | async-start | bytes 8388608
  580.6 20.5 %slice-start.2 = ((s8[16777216]{0:T(1024)(128)(4,1)}), s8[4194304]{0:T(1024)(128)(4,1)S(1)}, s32[]{:S(2)}) async-start(s8[16777216]{0:T(1024)(128)(4,1)} %bitcast.57), calls=%async_computation.6 | async-start | bytes 8388608
  593.8 4.6 copy-start.2
  593.8 9.0 %slice-start.3 = ((s8[16777216]{0:T(1024)(128)(4,1)}), s8[4194304]{0:T(1024)(128)(4,1)S(1)}, s32[]{:S(2)}) async-start(s8[16777216]{0:T(1024)(128)(4,1)} %bitcast.57), calls=%async_computation.7 | async-start | bytes 8388608
  602.8 6.2 %copy-start.1 = (bf16[128,4096]{1,0:T(8,128)(2,1)S(1)}, bf16[128,4096]{1,0:T(8,128)(2,1)}, u32[]{:S(2)}) copy-start(bf16[128,4096]{1,0:T(8,128)(2,1)} %param.7) | copy-start | bytes 3145732
  (3 other events, 4.1 us)
Sparse Core Ops, SparseCore 0:
  24.5 53.7 all-gather.1
  145.4 114.3 reduce-scatter.1
  282.1 298.4 all-reduce.2
